TPU v7x, 32 devices: a whole 2x2x4 slice. The times are simulated.
32 devices in a mesh: seq: 16 (over z, x, core), head: 2 (over y).
Axes of the slice: x: 2, y: 2, z: 4, core: 2. Of those that a mesh axis runs over, the one named last changes fastest.
Arguments:
- query: bfloat16 [1, 4096, 2048], P(None, 'seq', 'head'), may hold values from -210 to 210
- keys: bfloat16 [1, 4096, 512], P(None, 'seq', 'head'), may hold values from -7 to 7
- values: bfloat16 [1, 4096, 512], P(None, 'seq', 'head'), may hold values from -6 to 6
- grad_out: bfloat16 [1, 4096, 2048], P(None, 'seq', 'head'), may hold values from -6 to 6
- global_offset: int32 [1, 64], replicated, may hold values from 0 to 255, as said below
- owner: int32 [16], replicated, may hold values from 0 to 15, each once
- block_lists: int32 [1, 32, 3], P(None, 'seq'), may hold values from 0 to 31, as said below
Outputs:
- grad_query: bfloat16 [1, 4096, 2048], P(None, 'seq', 'head')
- grad_keys: bfloat16 [1, 4096, 512], P(None, 'seq', 'head')
- grad_values: bfloat16 [1, 4096, 512], P(None, 'seq', 'head')
Inputs may be any that keep to these rules, and one draw needn't show every extreme that they name: `block_lists`: row b of each layer lists b first, then 3 - 1 other distinct blocks within 2 blocks of b. `global_offset`: distinct within a layer. `owner`: each sequence shard appears once.
All inputs are finite; a program needn't handle non-finite values.
Results may differ from a plain program's by a relative error of at most 0.02.
Values may be sent and summed in bfloat16 or wider, within the bound.
A program may use at most 64 MiB of HBM per device.

v0:
```python
import jax
import jax.numpy as jnp
from jax import lax
from jax.sharding import PartitionSpec as P

HQ = 16
HK = 4
DH = 128
BLOCK = 128
REACH = 2
G = 64


def padded(block, sides, width):
    for axis, dim in sides:
        count = lax.axis_size(axis)
        forward = [(i, i + 1) for i in range(count - 1)]
        backward = [(target, source) for source, target in forward]
        low = lax.ppermute(
            lax.slice_in_dim(block, block.shape[dim] - width, None, axis=dim), axis, forward
        )
        high = lax.ppermute(lax.slice_in_dim(block, 0, width, axis=dim), axis, backward)
        block = jnp.concatenate([low, block, high], axis=dim)
    return block


def spread_2(array, axis, root):
    mine = lax.axis_index(axis) == root
    return lax.psum(jnp.where(mine, array, jnp.zeros_like(array)), axis)


def passed_along(value, axis, steps):
    count = lax.axis_size(axis)
    first, last = (max(0, -steps), min(count, count - steps))
    return lax.ppermute(value, axis, [(source, source + steps) for source in range(first, last)])


def scores(q_block, k_rows):
    return jnp.einsum(
        "tcgd,scd->cgts", q_block, k_rows, preferred_element_type=jnp.float32
    ) * DH ** (-0.5)


def backward(q_block, g_block, k_rows, v_rows, attn_probs, out_dot):
    attn_half = attn_probs.astype(jnp.bfloat16)
    grad_probs = jnp.einsum("tcgd,scd->cgts", g_block, v_rows, preferred_element_type=jnp.float32)
    grad_logits = (attn_probs * (grad_probs - out_dot[..., None])).astype(jnp.bfloat16)
    grad_q = jnp.einsum(
        "cgts,scd->tcgd", grad_logits, k_rows, preferred_element_type=jnp.float32
    ) * DH ** (-0.5)
    grad_k = jnp.einsum(
        "cgts,tcgd->scd", grad_logits, q_block, preferred_element_type=jnp.float32
    ) * DH ** (-0.5)
    grad_v = jnp.einsum("cgts,tcgd->scd", attn_half, g_block, preferred_element_type=jnp.float32)
    return (grad_q, grad_k, grad_v)


def attend(q_block, g_block, k_rows, v_rows):
    logits = scores(q_block, k_rows)
    top_logit = jnp.max(logits, axis=-1, keepdims=True)
    log_total = top_logit + jnp.log(jnp.sum(jnp.exp(logits - top_logit), axis=-1, keepdims=True))
    attn_probs = jnp.exp(logits - log_total)
    attn_half = attn_probs.astype(jnp.bfloat16)
    output = jnp.einsum(
        "cgts,scd->tcgd", attn_half, v_rows, preferred_element_type=jnp.float32
    ).astype(jnp.bfloat16)
    out_dot = jnp.einsum("tcgd,tcgd->cgt", g_block, output, preferred_element_type=jnp.float32)
    grad_q, grad_k, grad_v = backward(q_block, g_block, k_rows, v_rows, attn_probs, out_dot)
    return (grad_q, grad_k, grad_v, log_total[..., 0], out_dot)


def local(query, keys, values, grad_out, global_offset, owner, block_lists):
    row_count = query.shape[1]
    kv_width = keys.shape[2]
    heads_kv = kv_width // DH
    group_size = HQ // HK
    block_count = row_count // BLOCK
    listed = block_lists.shape[2]
    window_len = listed * BLOCK
    margin = REACH * BLOCK
    shard_index = lax.axis_index("seq")
    first_block = shard_index * block_count
    kv_pair = jnp.stack([keys[0], values[0]])
    widened = padded(kv_pair, (("seq", 1),), margin)
    picked = jnp.take(kv_pair, global_offset[0], axis=1)
    shared = spread_2(picked, "seq", owner[0])
    blocks = widened.reshape(2, block_count + 2 * REACH, BLOCK, heads_kv, DH)
    local_idx = block_lists[0] - first_block + REACH
    window = blocks[:, local_idx].reshape(2, block_count, window_len, heads_kv, DH)
    global_rows = jnp.broadcast_to(
        shared.reshape(2, 1, G, heads_kv, DH), (2, block_count, G, heads_kv, DH)
    )
    key_rows = jnp.concatenate([window, global_rows], axis=2)
    q_blocks = query[0].reshape(block_count, BLOCK, heads_kv, group_size, DH)
    g_blocks = grad_out[0].reshape(block_count, BLOCK, heads_kv, group_size, DH)
    grad_q, grad_k, grad_v, log_total, out_dot = jax.vmap(attend)(
        q_blocks, g_blocks, key_rows[0], key_rows[1]
    )
    grads_q = [grad_q.astype(jnp.bfloat16).reshape(row_count, -1)]
    partial_value = jnp.stack([grad_k[:, :window_len], grad_v[:, :window_len]]).reshape(
        2, block_count * listed, BLOCK, kv_width
    )
    spread = (
        jnp.zeros((2, block_count + 2 * REACH, BLOCK, kv_width), jnp.float32)
        .at[:, local_idx.reshape(-1)]
        .add(partial_value)
    )
    spread = spread.reshape(2, row_count + 2 * margin, kv_width)
    own_sums = spread[:, margin : margin + row_count]
    from_next = passed_along(spread[:, :margin], "seq", -1)
    from_prev = passed_along(spread[:, margin + row_count :], "seq", 1)
    own_sums = own_sums.at[:, :margin].add(from_prev).at[:, row_count - margin :].add(from_next)
    global_part = jnp.stack(
        [jnp.sum(grad_k[:, window_len:], axis=0), jnp.sum(grad_v[:, window_len:], axis=0)]
    )
    global_part = global_part.reshape(2, G, kv_width)
    owner_flag = (owner[0] == shard_index).astype(jnp.float32)
    share = lax.psum_scatter(global_part.reshape(-1), "seq", scatter_dimension=0, tiled=True)
    global_total = lax.all_gather(share, "seq", axis=0, tiled=True).reshape(2, G, kv_width)
    own_sums = own_sums.at[:, global_offset[0]].add(global_total * owner_flag)
    owned = [own_sums]
    grad_keys = jnp.stack([sums[0] for sums in owned]).astype(jnp.bfloat16)
    grad_values = jnp.stack([sums[1] for sums in owned]).astype(jnp.bfloat16)
    return (jnp.stack(grads_q), grad_keys, grad_values)


def solution(mesh):
    return jax.shard_map(
        local,
        mesh=mesh,
        in_specs=(
            P(None, "seq", "head"),
            P(None, "seq", "head"),
            P(None, "seq", "head"),
            P(None, "seq", "head"),
            P(),
            P(),
            P(None, "seq", None),
        ),
        out_specs=(P(None, "seq", "head"), P(None, "seq", "head"), P(None, "seq", "head")),
        check_vma=False,
    )
```

profile of v0, /device:TPU:0, one launch (start us, length us, event | category | flops | bytes accessed | tf_op | source)
XLA Modules:
  0.0 249.0 jit_solution(18314176029845374509)
XLA Ops:
  7.2 1.1 copy.93
  8.3 1.1 copy.94
  10.1 2.4 collective-permute-start
  12.5 1.3 collective-permute-start.1
  14.4 0.7 compare_and_fusion
  15.1 0.7 gather_fusion.1
  17.4 0.7 compare_select_fusion
  18.8 1.4 reshape_squeeze.6
  20.2 1.4 reshape_squeeze.7
  23.1 1.3 pad_maximum_fusion
  25.1 0.7 gather_fusion
  25.9 82.3 %all-reduce.4.cloned.1.call-done = bf16[2,64,2,128]{3,1,2,0:T(8,128)(2,1)} async-done(((bf16[2,64,2,128]{3,1,2,0:T(8,128)(2,1)}), bf16[2,64,2,128]{3,1,2,0:T(8,128)(2,1)}) %all-reduce.4.cloned.1.call-update) | async-done | bytes 65552 | tf_op jit(solution)/shard_map/psum | solution.py:29
  108.2 0.9 broadcast_in_dim.33
  110.4 1.8 fusion.10
  112.2 0.7 convolution_bitcast_fusion
  112.9 0.9 slice.96
  113.9 1.7 copy.121
  115.6 0.9 multiply_reduce_fusion
  116.5 3.1 %fusion.1 = bf16[2,2,4,128,448]{3,4,2,1,0:T(8,128)(2,1)S(1)} fusion(f32[2,2,448,128,4]{3,2,4,1,0:T(8,128)} %copy-done, f32[2,2,4,128]{3,2,1,0:T(4,128)S(1)} %copy.122, f32[2,2,4,128]{3,2,1,0:T(4,128)S(1)} %bitcast.113, bf16[2,128,2,4,128]{4,3,2,1,0:T(4,128)(2,1)S(1)} %reshape_squeeze.7, bf16[2,2,64,2,128]{4,2,3,1,0:T(8,128)(2,1)S(1)} %broadcast_in_dim.33, ...), kind=kOutput, calls=%fused_computation.6 | convolution fusion | flops 240386048 | bytes 6963200 | tf_op jit(solution)/shard_map/vmap(tcgd,scd->cgts)/dot_general | solution.py:46
  120.4 1.3 fusion.11
  121.7 0.8 copy.110
  125.3 1.8 scatter_fusion
  127.8 2.1 collective-permute-start.2
  130.2 1.3 collective-permute-start.3
  131.9 1.2 stack_reshape.3
  133.0 79.5 %all-reduce.6.cloned.1.call-done = f32[32768]{0:T(1024)} async-done(((f32[32768]{0:T(1024)}), f32[32768]{0:T(1024)}) %all-reduce.6.cloned.1.call-update) | async-done | bytes 131088
  212.5 0.7 dynamic-slice.11
  213.2 22.3 %all_gather.3 = f32[32768]{0:T(1024)S(1)} all-gather(f32[2048]{0:T(1024)S(1)} %dynamic-slice.11), channel_id=1, replica_groups=mesh['seq'=16,'head'=2] {'seq'}, dimensions={0}, use_global_device_ids=true | all-gather | bytes 139264 | tf_op jit(solution)/shard_map/all_gather | solution.py:119
  235.7 1.7 fusion.12
  237.4 2.9 %scatter_fusion.1 = f32[2,256,256]{2,0,1:T(2,128)S(1)} fusion(f32[2,256,256]{2,0,1:T(2,128)S(1)} %fusion.12, s32[64]{0:T(128)S(1)} %fusion.28, f32[64,2,256]{2,1,0:T(2,128)S(1)} %copy.111), kind=kCustom, calls=%fused_computation.3 | custom fusion | flops 32768 | bytes 393472 | tf_op jit(solution)/shard_map/scatter-add | solution.py:120
  240.8 0.7 copy.112
  241.5 0.7 copy.113
  (56 shorter events, 10.7 us)
Async XLA Ops:
  7.2 14.7 %copy-start.3 = (u32[32]{0:T(128)S(1)}, u32[32]{0:T(128)}, u32[]{:S(2)}) copy-start(u32[32]{0:T(128)} %constant.115) | copy-start | bytes 388
  7.2 101.0 %all-reduce.4.cloned.1.call-start = ((), (), s32[]{:S(2)}) async-start(), calls=%async_computation | async-start | bytes 131072 | tf_op jit(solution)/shard_map/psum | solution.py:29
  10.1 13.0 %collective-permute-start = (bf16[2,256,256]{2,0,1:T(2,128)(2,1)S(1)}, bf16[2,256,256]{2,0,1:T(2,128)(2,1)S(1)}, u32[]{:S(2)}, u32[]{:S(2)}) collective-permute-start(bf16[2,256,256]{2,0,1:T(2,128)(2,1)S(1)} %pad_maximum_fusion.2), channel_id=1, source_target_pairs={{0,2},{2,4},{4,6},{6,8},{8,10},{10,12},{12,14},{14,16},{16,18},{18... | collective-permute-start | bytes 786440 | tf_op jit(solution)/shard_map/ppermute | solution.py:19
  12.5 10.6 %collective-permute-start.1 = (bf16[2,256,256]{2,0,1:T(2,128)(2,1)S(1)}, bf16[2,256,256]{2,0,1:T(2,128)(2,1)S(1)}, u32[]{:S(2)}, u32[]{:S(2)}) collective-permute-start(bf16[2,256,256]{2,0,1:T(2,128)(2,1)S(1)} %pad_maximum_fusion.2), channel_id=1, source_target_pairs={{2,0},{4,2},{6,4},{8,6},{10,8},{12,10},{14,12},{16,14},{18,16},{20... | collective-permute-start | bytes 786440 | tf_op jit(solution)/shard_map/ppermute | solution.py:22
  17.4 195.2 %all-reduce.6.cloned.1.call-start = ((), (), s32[]{:S(2)}) async-start(), calls=%async_computation.1 | async-start | bytes 262144
  109.7 2.5 copy-start
  120.3 2.2 copy-start.1
  127.2 4.4 %copy-start.2 = (bf16[2,128,2,4,128]{1,4,3,2,0:T(8,128)(2,1)S(1)}, bf16[2,128,2,4,128]{1,4,3,2,0:T(8,128)(2,1)}, u32[]{:S(2)}) copy-start(bf16[2,128,2,4,128]{1,4,3,2,0:T(8,128)(2,1)} %fusion.11) | copy-start | bytes 1572868
  127.8 107.9 %collective-permute-start.2 = (f32[2,256,256]{2,0,1:T(2,128)S(1)}, f32[2,256,256]{2,0,1:T(2,128)S(1)}, u32[]{:S(2)}, u32[]{:S(2)}) collective-permute-start(f32[2,256,256]{2,0,1:T(2,128)S(1)} %copy.128), channel_id=1, source_target_pairs={{0,2},{2,4},{4,6},{6,8},{8,10},{10,12},{12,14},{14,16},{16,18},{18... | collective-permute-start | bytes 1572872 | tf_op jit(solution)/shard_map/ppermute | solution.py:35
  130.2 105.4 %collective-permute-start.3 = (f32[2,256,256]{2,0,1:T(2,128)S(1)}, f32[2,256,256]{2,0,1:T(2,128)}, u32[]{:S(2)}, u32[]{:S(2)}) collective-permute-start(f32[2,256,256]{2,0,1:T(2,128)S(1)} %copy.129), channel_id=1, source_target_pairs={{2,0},{4,2},{6,4},{8,6},{10,8},{12,10},{14,12},{16,14},{18,16},{20... | collective-permute-start | bytes 1572872 | tf_op jit(solution)/shard_map/ppermute | solution.py:35
Sparse Core Ops, SparseCore 0:
  17.5 90.6 all-reduce.3
  122.6 89.8 all-reduce.5
where the time goes:
time: 250 us; the launch traced here: 249 us
  waiting for transfers between devices  162 us (65%)
  blocking collectives  22.3 us (9%)
  local copies, waits for them, and re-layouts  20.8 us (8%)
  between operations  16.4 us (7%)
  other arithmetic  12.2 us (5%)
  matrix products  8.23 us (3%)
  starting transfers between devices  7.13 us (3%)
    psum x1, waiting for transfers between devices, spread_2(): return lax.psum(jnp.where(mine, array, jnp.zeros_like(array)), axis)  82.3 us
    unnamed x3, waiting for transfers between devices  79.5 us
    all_gather x1, blocking collectives, local(): lax.all_gather(share, 'seq', axis=0, tiled=True).reshape(2, G, kv_width)  22.3 us
    unnamed x17, local copies, waits for them, and re-layouts  7.34 us
  transfers between devices with their start and end apart: 6, of which 2 were waited for; matrix products, arithmetic and copies ran while one was open for 7% of the time, Pallas kernels for 0%

commit v1 on v0

v1 whole, which is shorter than its diff:
```python
import functools

import jax
import jax.numpy as jnp
from jax import lax
from jax.experimental import pallas as pl
from jax.experimental.pallas import tpu as pltpu
from jax.sharding import PartitionSpec as P

HQ = 16
HK = 4
DH = 128
BLOCK = 128
REACH = 2
PIECE = 16
LOG2E = 1.4426950408889634
F32 = jnp.float32
BF16 = jnp.bfloat16


def nt(a, b):
    return lax.dot_general(a, b, (((1,), (1,)), ((), ())), preferred_element_type=F32)


def nn(a, b):
    return lax.dot_general(a, b, (((1,), (0,)), ((), ())), preferred_element_type=F32)


def kernel(
    n, heads, group, nb, listed, gtok,
    owner_ref, lists_ref, goff_ref, q_hbm, k_hbm, v_hbm, g_hbm,
    dq_ref, dk_ref, dv_ref,
    qv, gv, gsend, hub_in, hub_out, gall, gpart, hub2_in, hub2_out, gall2,
    wslot, own, sback, rback, load_sem, big_sem, ks_sem, kr_sem, gs_sem, gr_sem, hs_sem, hr_sem,
    *kvw,
):
    me = lax.axis_index("seq")
    rpp = gtok // PIECE
    pieces = 2 * heads * rpp
    rows = nb * BLOCK
    src_refs = (k_hbm, v_hbm)

    loads = []
    for t in range(2):
        for c in range(heads):
            for i in range(nb):
                cp = pltpu.make_async_copy(
                    src_refs[t].at[0, pl.ds(i * BLOCK, BLOCK), pl.ds(c * DH, DH)],
                    kvw[t * heads + c].at[REACH + i],
                    load_sem.at[(t * heads + c) * nb + i],
                )
                cp.start()
                loads.append(cp)
    cq = pltpu.make_async_copy(q_hbm.at[0], qv, big_sem.at[0])
    cg = pltpu.make_async_copy(g_hbm.at[0], gv, big_sem.at[1])
    cq.start()
    cg.start()

    barrier = pltpu.get_barrier_semaphore()

    @pl.loop(1, n)
    def _(i):
        pl.semaphore_signal(
            barrier, inc=1, device_id={"seq": lax.rem(me + i, n)}, device_id_type=pl.DeviceIdType.MESH
        )

    for cp in loads:
        cp.wait()

    hot = lax.broadcasted_iota(jnp.int32, (rows, gtok), 0) == goff_ref[...]
    hot = jnp.where(hot, 1.0, 0.0).astype(BF16)
    for t in range(2):
        for c in range(heads):
            mine = kvw[t * heads + c][REACH : REACH + nb].reshape(rows, DH)
            got = lax.dot_general(hot, mine, (((0,), (0,)), ((), ())), preferred_element_type=F32)
            base = (t * heads + c) * rpp
            gsend[base : base + rpp] = got.astype(BF16).reshape(rpp, PIECE, DH)
    zeros_kv = jnp.zeros((REACH, BLOCK, DH), BF16)

    @pl.when(me == 0)
    def _():
        for ref in kvw:
            ref[0:REACH] = zeros_kv
        rback[0] = jnp.zeros(rback.shape[1:], BF16)

    @pl.when(me == n - 1)
    def _():
        for ref in kvw:
            ref[REACH + nb : REACH + nb + REACH] = zeros_kv
        rback[1] = jnp.zeros(rback.shape[1:], BF16)

    zero_tile = jnp.zeros((nb, 2, BLOCK, DH), F32)
    wslot[:, listed] = zero_tile

    pl.semaphore_wait(barrier, n - 1)

    def remote(src, dst, s_sem, r_sem, target):
        return pltpu.make_async_remote_copy(
            src_ref=src, dst_ref=dst, send_sem=s_sem, recv_sem=r_sem,
            device_id={"seq": target}, device_id_type=pl.DeviceIdType.MESH,
        )

    def hub_send(src, dst, s_sem, r_sem, j):
        @pl.when(j != me)
        def _():
            remote(src.at[j], dst.at[me], s_sem, r_sem, j).start()

    def drain(ref, count, sem):
        part = ref.at[pl.ds(0, count)]
        pltpu.make_async_copy(part, part, sem).wait()

    @pl.loop(0, pieces)
    def _(i):
        hub_send(gsend, hub_in, hs_sem.at[0], hr_sem.at[0], lax.rem(me + i, pieces))

    def halo(direction, c, t):
        idx = (direction * heads + c) * 2 + t
        ref = kvw[t * heads + c]
        if direction == 0:
            src, dst, target = ref.at[pl.ds(nb, REACH)], ref.at[pl.ds(0, REACH)], me + 1
        else:
            src, dst, target = ref.at[pl.ds(REACH, REACH)], ref.at[pl.ds(REACH + nb, REACH)], me - 1
        return remote(src, dst, ks_sem.at[idx], kr_sem.at[idx], target)

    def back(direction, c):
        idx = direction * heads + c
        target = me + 1 if direction == 0 else me - 1
        return remote(
            sback.at[direction, c], rback.at[direction, c], gs_sem.at[idx], gr_sem.at[idx], target
        )

    def each(direction, receiving, what):
        up = (direction == 0) != receiving
        cond = me < n - 1 if up else me > 0
        pl.when(cond)(what)

    for c in range(heads):
        for t in range(2):
            for d in range(2):
                each(d, False, lambda d=d, c=c, t=t: halo(d, c, t).start())

    @pl.when(me < pieces)
    def _():
        hub_in[me] = gsend[me]
        drain(hub_in, n - 1, hr_sem.at[0])
        pick = hub_in[owner_ref[0]]
        hub_out[...] = pick
        gall[me] = pick

        @pl.loop(1, n)
        def _(i):
            remote(hub_out, gall.at[me], hs_sem.at[1], hr_sem.at[1], lax.rem(me + i, n)).start()

        drain(gall, pieces - 1, hr_sem.at[1])

    @pl.when(me >= pieces)
    def _():
        drain(gall, pieces, hr_sem.at[1])

    cq.wait()
    cg.wait()
    scale = DH ** (-0.5)
    local_idx = [
        [
            jnp.clip(lists_ref[0, b, l] - me * nb + REACH, 0, nb + 2 * REACH - 1)
            for l in range(listed)
        ]
        for b in range(nb)
    ]
    win = listed * BLOCK
    for c in range(heads):
        for t in range(2):
            for d in range(2):
                each(d, True, lambda d=d, c=c, t=t: halo(d, c, t).wait_recv())
        kref, vref = kvw[c], kvw[heads + c]
        kg = gall[c * rpp : (c + 1) * rpp].reshape(gtok, DH)
        vg = gall[(heads + c) * rpp : (heads + c + 1) * rpp].reshape(gtok, DH)
        glob = [None, None]
        for b in range(nb):
            ks = jnp.concatenate([kref[local_idx[b][l]] for l in range(listed)] + [kg], axis=0)
            vs = jnp.concatenate([vref[local_idx[b][l]] for l in range(listed)] + [vg], axis=0)
            rsl = slice(b * BLOCK, (b + 1) * BLOCK)
            cols = [slice((c * group + i) * DH, (c * group + i + 1) * DH) for i in range(group)]
            qs = jnp.concatenate([qv[rsl, s] for s in cols], axis=0)
            gs = jnp.concatenate([gv[rsl, s] for s in cols], axis=0)
            st = nt(ks, qs)
            dp = nt(vs, gs)
            top = jnp.max(st, axis=0, keepdims=True)
            ex = jnp.exp2((st - top) * (scale * LOG2E))
            inv = 1.0 / jnp.sum(ex, axis=0, keepdims=True)
            dot = jnp.sum(ex * dp, axis=0, keepdims=True) * inv
            pr = ex * inv
            half = pr.astype(BF16)
            ds = (pr * (dp - dot)).astype(BF16)
            dv = nn(half, gs)
            dk = nn(ds, qs) * scale
            dqt = nn(ks.T, ds) * scale
            dq = dqt.T.astype(BF16)
            for i, s in enumerate(cols):
                dq_ref[0, rsl, s] = dq[i * BLOCK : (i + 1) * BLOCK]
            for t, val in enumerate((dk, dv)):
                for l in range(listed):
                    wslot[b, l, t] = val[l * BLOCK : (l + 1) * BLOCK]
                part = val[win:]
                glob[t] = part if glob[t] is None else glob[t] + part
        for t in range(2):
            base = (t * heads + c) * rpp
            gpart[base : base + rpp] = glob[t].astype(BF16).reshape(rpp, PIECE, DH)
        for dst in range(nb + 2 * REACH):
            total = None
            for b in range(nb):
                if not b <= dst <= b + 2 * REACH:
                    continue
                slot = jnp.int32(listed)
                for l in range(listed):
                    slot = jnp.where(local_idx[b][l] == dst, l, slot)
                term = wslot[b, slot]
                total = term if total is None else total + term
            if dst < REACH:
                sback[1, c, dst] = total.astype(BF16)
            elif dst < REACH + nb:
                own[c, dst - REACH] = total
            else:
                sback[0, c, dst - REACH - nb] = total.astype(BF16)
        for d in range(2):
            each(d, False, lambda d=d, c=c: back(d, c).start())
        for t in range(2):
            for r in range(rpp):
                hub_send(gpart, hub2_in, hs_sem.at[2], hr_sem.at[2], (t * heads + c) * rpp + r)

    @pl.when(me < pieces)
    def _():
        hub2_in[me] = gpart[me]
        drain(hub2_in, n - 1, hr_sem.at[2])
        total = jnp.sum(hub2_in[...].astype(F32), axis=0).astype(BF16)
        hub2_out[...] = total
        gall2[me] = total

        @pl.loop(1, n)
        def _(i):
            remote(hub2_out, gall2.at[me], hs_sem.at[3], hr_sem.at[3], lax.rem(me + i, n)).start()

        drain(gall2, pieces - 1, hr_sem.at[3])

    @pl.when(me >= pieces)
    def _():
        drain(gall2, pieces, hr_sem.at[3])

    flag = jnp.where(owner_ref[0] == me, 1.0, 0.0)
    for c in range(heads):
        for d in range(2):
            each(d, True, lambda d=d, c=c: back(d, c).wait_recv())
        for t, out in enumerate((dk_ref, dv_ref)):
            base = (t * heads + c) * rpp
            extra = nn(hot, gall2[base : base + rpp].reshape(gtok, DH)) * flag
            for i in range(nb):
                rsl = slice(i * BLOCK, (i + 1) * BLOCK)
                total = own[c, i, t] + extra[rsl]
                total = total + rback[0, c, i, t].astype(F32) + rback[1, c, i, t].astype(F32)
                out[0, rsl, c * DH : (c + 1) * DH] = total.astype(BF16)

    for c in range(heads):
        for d in range(2):
            for t in range(2):
                each(d, False, lambda d=d, c=c, t=t: halo(d, c, t).wait_send())
            each(d, False, lambda d=d, c=c: back(d, c).wait_send())

    @pl.when(me < pieces)
    def _():
        drain(gsend, pieces - 1, hs_sem.at[0])
        drain(gpart, pieces - 1, hs_sem.at[2])
        drain(hub_in, n - 1, hs_sem.at[1])
        drain(hub2_in, n - 1, hs_sem.at[3])

    @pl.when(me >= pieces)
    def _():
        drain(gsend, pieces, hs_sem.at[0])
        drain(gpart, pieces, hs_sem.at[2])


def solution(mesh):
    n = mesh.shape["seq"]

    def local(query, keys, values, grad_out, global_offset, owner, block_lists):
        rows, qw = query.shape[1:]
        kw = keys.shape[2]
        heads = kw // DH
        group = HQ // HK
        nb = rows // BLOCK
        listed = block_lists.shape[2]
        gtok = global_offset.shape[1]
        pieces = 2 * heads * gtok // PIECE
        wide = nb + 2 * REACH
        assert nb == REACH and n >= pieces
        vm = pl.BlockSpec(memory_space=pltpu.VMEM)
        sm = pl.BlockSpec(memory_space=pltpu.SMEM)
        hb = pl.BlockSpec(memory_space=pl.ANY)
        return pl.pallas_call(
            functools.partial(kernel, n, heads, group, nb, listed, gtok),
            out_shape=(
                jax.ShapeDtypeStruct(query.shape, BF16),
                jax.ShapeDtypeStruct(keys.shape, BF16),
                jax.ShapeDtypeStruct(values.shape, BF16),
            ),
            in_specs=[sm, sm, vm, hb, hb, hb, hb],
            out_specs=(vm, vm, vm),
            scratch_shapes=[
                pltpu.VMEM((rows, qw), BF16),
                pltpu.VMEM((rows, qw), BF16),
                pltpu.VMEM((pieces, PIECE, DH), BF16),
                pltpu.VMEM((n, PIECE, DH), BF16),
                pltpu.VMEM((PIECE, DH), BF16),
                pltpu.VMEM((pieces, PIECE, DH), BF16),
                pltpu.VMEM((pieces, PIECE, DH), BF16),
                pltpu.VMEM((n, PIECE, DH), BF16),
                pltpu.VMEM((PIECE, DH), BF16),
                pltpu.VMEM((pieces, PIECE, DH), BF16),
                pltpu.VMEM((nb, listed + 1, 2, BLOCK, DH), F32),
                pltpu.VMEM((heads, nb, 2, BLOCK, DH), F32),
                pltpu.VMEM((2, heads, REACH, 2, BLOCK, DH), BF16),
                pltpu.VMEM((2, heads, REACH, 2, BLOCK, DH), BF16),
                pltpu.SemaphoreType.DMA((2 * heads * nb,)),
                pltpu.SemaphoreType.DMA((2,)),
                pltpu.SemaphoreType.DMA((4 * heads,)),
                pltpu.SemaphoreType.DMA((4 * heads,)),
                pltpu.SemaphoreType.DMA((2 * heads,)),
                pltpu.SemaphoreType.DMA((2 * heads,)),
                pltpu.SemaphoreType.DMA((4,)),
                pltpu.SemaphoreType.DMA((4,)),
            ]
            + [pltpu.VMEM((wide, BLOCK, DH), BF16)] * (2 * heads),
            compiler_params=pltpu.CompilerParams(collective_id=0, has_side_effects=True),
        )(owner, block_lists, global_offset, query, keys, values, grad_out)

    return jax.shard_map(
        local,
        mesh=mesh,
        in_specs=(
            P(None, "seq", "head"),
            P(None, "seq", "head"),
            P(None, "seq", "head"),
            P(None, "seq", "head"),
            P(),
            P(),
            P(None, "seq", None),
        ),
        out_specs=(P(None, "seq", "head"), P(None, "seq", "head"), P(None, "seq", "head")),
        check_vma=False,
    )
```

time: 250 us -> 35 us (0.14)
  waiting for transfers between devices: 162 us -> 0 us
  Pallas kernels: 0 us -> 30.6 us
  blocking collectives: 22.3 us -> 0 us
  local copies, waits for them, and re-layouts: 20.8 us -> 3.51 us
  between operations: 16.4 us -> 0.65 us
  other arithmetic: 12.2 us -> 0 us
  matrix products: 8.23 us -> 0 us
  starting transfers between devices: 7.13 us -> 0 us
    psum x1 -> x0, waiting for transfers between devices: 82.3 us -> none  [spread_2(): return lax.psum(jnp.where(mine, array, jnp.zeros_like(array)), axis)]
    unnamed x3 -> x0, waiting for transfers between devices: 79.5 us -> none
    pallas_call x0 -> x1, Pallas kernels: none -> 30.6 us  [local(): pl.pallas_call(functools.partial(kernel, n, heads, group, nb, listed, gto...]
    all_gather x1 -> x0, blocking collectives: 22.3 us -> none  [local(): lax.all_gather(share, 'seq', axis=0, tiled=True).reshape(2, G, kv_width)]
    dot_general x6 -> x0, matrix products: 8.23 us -> none  [the longest x1 3.11 us: backward(): jnp.einsum('tcgd,scd->cgts', g_block, v_rows, preferred_element_type=jnp....]
    ppermute x4 -> x0, starting transfers between devices: 7.05 us -> none  [the longest x2 3.35 us: passed_along(): lax.ppermute(value, axis, [(source, source + steps) for source in range(f...]
    another operation x7 -> x0, local copies, waits for them, and re-layouts: 6.1 us -> none  [the longest x1 1.41 us: local(): g_blocks = grad_out[0].reshape(block_count, BLOCK, heads_kv, group_size, DH)]
    scatter-add x2 -> x0, other arithmetic: 4.66 us -> none  [the longest x1 2.85 us: local(): own_sums = own_sums.at[:, global_offset[0]].add(global_total * owner_flag)]
  transfers between devices with their start and end apart: 6 -> 0, of which waited for: 2 -> 0; matrix products, arithmetic and copies ran while one was open for 7% -> 0% of each run, Pallas kernels for 0% -> 0%
where the time goes in v1:
time: 35 us; the launch traced here: 34.8 us
  Pallas kernels  30.6 us (87%)
  local copies, waits for them, and re-layouts  3.51 us (10%)
  between operations  0.65 us (2%)
    pallas_call x1, Pallas kernels, local(): pl.pallas_call(functools.partial(kernel, n, heads, group, nb, listed, gto...  30.6 us
    unnamed x7, local copies, waits for them, and re-layouts  3.51 us

profile of v1, /device:TPU:0, one launch (start us, length us, event | category | flops | bytes accessed | tf_op | source)
XLA Modules:
  0.0 34.8 jit_solution(7615056321010426870)
XLA Ops:
  0.6 30.6 %shard_map.94 = (bf16[1,256,1024]{2,1,0:T(8,128)(2,1)}, bf16[1,256,256]{2,1,0:T(8,128)(2,1)}, bf16[1,256,256]{2,1,0:T(8,128)(2,1)}) custom-call(s32[16]{0:T(128)} %owner_ref.1, s32[1,2,3]{2,1,0:T(2,128)} %lists_ref.1, s32[1,64]{1,0:T(1,128)} %goff_ref.1, bf16[1,256,1024]{2,1,0:T(8,128)(2,1)} %q_hbm.1, bf16[1,256,256]{2,1,0:T(8,128)(2,1)} %k_hbm.1, ...), custom_call_target="tpu_custom_call" | custom-call | tf_op jit(solution)/shard_map/pallas_call | solution.py:298
  31.3 0.0 copy-start.1
  31.3 1.9 %copy.13 = bf16[1,256,1024]{2,1,0:T(8,128)(2,1)} copy(bf16[1,256,1024]{2,1,0:T(8,128)(2,1)} %get-tuple-element.6) | data formatting | bytes 1048576
  33.2 0.0 copy-done.1
  33.2 0.0 copy-start
  33.2 0.7 %copy.14 = bf16[1,256,256]{2,1,0:T(8,128)(2,1)} copy(bf16[1,256,256]{2,1,0:T(8,128)(2,1)S(1)} %copy-done.1) | data formatting | bytes 262144
  33.9 0.3 copy-done
  34.2 0.7 %copy.15 = bf16[1,256,256]{2,1,0:T(8,128)(2,1)} copy(bf16[1,256,256]{2,1,0:T(8,128)(2,1)S(1)} %copy-done) | data formatting | bytes 262144
Async XLA Ops:
  31.3 1.9 %copy-start.1 = (bf16[1,256,256]{2,1,0:T(8,128)(2,1)S(1)}, bf16[1,256,256]{2,1,0:T(8,128)(2,1)}, u32[]{:S(2)}) copy-start(bf16[1,256,256]{2,1,0:T(8,128)(2,1)} %get-tuple-element.7) | copy-start | bytes 393220
  33.2 1.0 %copy-start = (bf16[1,256,256]{2,1,0:T(8,128)(2,1)S(1)}, bf16[1,256,256]{2,1,0:T(8,128)(2,1)}, u32[]{:S(2)}) copy-start(bf16[1,256,256]{2,1,0:T(8,128)(2,1)} %get-tuple-element.8) | copy-start | bytes 393220

commit v2 on v1

--- a/solution.py
+++ b/solution.py
@@ -12,7 +12,7 @@
 DH = 128
 BLOCK = 128
 REACH = 2
-PIECE = 16
+PIECE = 32
 LOG2E = 1.4426950408889634
 F32 = jnp.float32
 BF16 = jnp.bfloat16
@@ -31,7 +31,7 @@
     owner_ref, lists_ref, goff_ref, q_hbm, k_hbm, v_hbm, g_hbm,
     dq_ref, dk_ref, dv_ref,
     qv, gv, gsend, hub_in, hub_out, gall, gpart, hub2_in, hub2_out, gall2,
-    wslot, own, sback, rback, load_sem, big_sem, ks_sem, kr_sem, gs_sem, gr_sem, hs_sem, hr_sem,
+    keep_ex, keep_dp, keep_ds, wslot, own, sback, rback, load_sem, big_sem, ks_sem, kr_sem, gs_sem, gr_sem, hs_sem, hr_sem,
     *kvw,
 ):
     me = lax.axis_index("seq")
@@ -58,11 +58,21 @@
 
     barrier = pltpu.get_barrier_semaphore()
 
+    first = (n - pieces) // 2
+    hub = me - first
+
+    def hubbed(i):
+        return (i >= first) & (i < first + pieces)
+
     @pl.loop(1, n)
     def _(i):
-        pl.semaphore_signal(
-            barrier, inc=1, device_id={"seq": lax.rem(me + i, n)}, device_id_type=pl.DeviceIdType.MESH
-        )
+        other = lax.rem(me + i, n)
+
+        @pl.when(hubbed(me) | hubbed(other) | (other == me + 1) | (other == me - 1))
+        def _():
+            pl.semaphore_signal(
+                barrier, inc=1, device_id={"seq": other}, device_id_type=pl.DeviceIdType.MESH
+            )
 
     for cp in loads:
         cp.wait()
@@ -92,7 +102,9 @@
     zero_tile = jnp.zeros((nb, 2, BLOCK, DH), F32)
     wslot[:, listed] = zero_tile
 
-    pl.semaphore_wait(barrier, n - 1)
+    below = jnp.where((me > 0) & ~hubbed(me - 1), 1, 0)
+    above = jnp.where((me < n - 1) & ~hubbed(me + 1), 1, 0)
+    pl.semaphore_wait(barrier, jnp.where(hubbed(me), n - 1, pieces + below + above))
 
     def remote(src, dst, s_sem, r_sem, target):
         return pltpu.make_async_remote_copy(
@@ -101,9 +113,9 @@
         )
 
     def hub_send(src, dst, s_sem, r_sem, j):
-        @pl.when(j != me)
+        @pl.when(j != hub)
         def _():
-            remote(src.at[j], dst.at[me], s_sem, r_sem, j).start()
+            remote(src.at[j], dst.at[me], s_sem, r_sem, first + j).start()
 
     def drain(ref, count, sem):
         part = ref.at[pl.ds(0, count)]
@@ -139,27 +151,22 @@
             for d in range(2):
                 each(d, False, lambda d=d, c=c, t=t: halo(d, c, t).start())
 
-    @pl.when(me < pieces)
-    def _():
-        hub_in[me] = gsend[me]
+    @pl.when(hubbed(me))
+    def _():
+        hub_in[me] = gsend[hub]
         drain(hub_in, n - 1, hr_sem.at[0])
         pick = hub_in[owner_ref[0]]
         hub_out[...] = pick
-        gall[me] = pick
+        gall[hub] = pick
 
         @pl.loop(1, n)
         def _(i):
-            remote(hub_out, gall.at[me], hs_sem.at[1], hr_sem.at[1], lax.rem(me + i, n)).start()
-
-        drain(gall, pieces - 1, hr_sem.at[1])
-
-    @pl.when(me >= pieces)
-    def _():
-        drain(gall, pieces, hr_sem.at[1])
+            remote(hub_out, gall.at[hub], hs_sem.at[1], hr_sem.at[1], lax.rem(me + i, n)).start()
 
     cq.wait()
     cg.wait()
     scale = DH ** (-0.5)
+    fold = scale * LOG2E
     local_idx = [
         [
             jnp.clip(lists_ref[0, b, l] - me * nb + REACH, 0, nb + 2 * REACH - 1)
@@ -167,45 +174,90 @@
         ]
         for b in range(nb)
     ]
-    win = listed * BLOCK
+
+    def listed_rows(t, c, b):
+        return jnp.concatenate([kvw[t * heads + c][local_idx[b][l]] for l in range(listed)], axis=0)
+
+    def global_rows(ref, t, c):
+        base = (t * heads + c) * rpp
+        return ref[base : base + rpp].reshape(gtok, DH)
+
+    def columns(c):
+        return [slice((c * group + i) * DH, (c * group + i + 1) * DH) for i in range(group)]
+
+    def stacked(ref, c, b):
+        rsl = slice(b * BLOCK, (b + 1) * BLOCK)
+        return jnp.concatenate([ref[rsl, s] for s in columns(c)], axis=0)
+
+    stats = {}
     for c in range(heads):
         for t in range(2):
             for d in range(2):
                 each(d, True, lambda d=d, c=c, t=t: halo(d, c, t).wait_recv())
-        kref, vref = kvw[c], kvw[heads + c]
-        kg = gall[c * rpp : (c + 1) * rpp].reshape(gtok, DH)
-        vg = gall[(heads + c) * rpp : (heads + c + 1) * rpp].reshape(gtok, DH)
+        for b in range(nb):
+            st = nt(listed_rows(0, c, b), stacked(qv, c, b))
+            dp = nt(listed_rows(1, c, b), stacked(gv, c, b))
+            top = jnp.max(st, axis=0, keepdims=True)
+            ex = jnp.exp2((st - top) * fold)
+            keep_ex[c, b] = ex
+            keep_dp[c, b] = dp
+            stats[c, b] = (
+                top,
+                jnp.sum(ex, axis=0, keepdims=True),
+                jnp.sum(ex * dp, axis=0, keepdims=True),
+            )
+
+    @pl.when(hubbed(me))
+    def _():
+        drain(gall, pieces - 1, hr_sem.at[1])
+
+    @pl.when(~hubbed(me))
+    def _():
+        drain(gall, pieces, hr_sem.at[1])
+
+    for c in range(heads):
+        kg, vg = global_rows(gall, 0, c), global_rows(gall, 1, c)
         glob = [None, None]
         for b in range(nb):
-            ks = jnp.concatenate([kref[local_idx[b][l]] for l in range(listed)] + [kg], axis=0)
-            vs = jnp.concatenate([vref[local_idx[b][l]] for l in range(listed)] + [vg], axis=0)
-            rsl = slice(b * BLOCK, (b + 1) * BLOCK)
-            cols = [slice((c * group + i) * DH, (c * group + i + 1) * DH) for i in range(group)]
-            qs = jnp.concatenate([qv[rsl, s] for s in cols], axis=0)
-            gs = jnp.concatenate([gv[rsl, s] for s in cols], axis=0)
-            st = nt(ks, qs)
-            dp = nt(vs, gs)
-            top = jnp.max(st, axis=0, keepdims=True)
-            ex = jnp.exp2((st - top) * (scale * LOG2E))
-            inv = 1.0 / jnp.sum(ex, axis=0, keepdims=True)
-            dot = jnp.sum(ex * dp, axis=0, keepdims=True) * inv
+            qs, gs = stacked(qv, c, b), stacked(gv, c, b)
+            st = nt(kg, qs)
+            dp = nt(vg, gs)
+            top_w, sum_w, dot_w = stats[c, b]
+            top = jnp.maximum(top_w, jnp.max(st, axis=0, keepdims=True))
+            ex = jnp.exp2((st - top) * fold)
+            shrink = jnp.exp2((top_w - top) * fold)
+            inv = 1.0 / (sum_w * shrink + jnp.sum(ex, axis=0, keepdims=True))
+            dot = (dot_w * shrink + jnp.sum(ex * dp, axis=0, keepdims=True)) * inv
             pr = ex * inv
-            half = pr.astype(BF16)
             ds = (pr * (dp - dot)).astype(BF16)
-            dv = nn(half, gs)
-            dk = nn(ds, qs) * scale
-            dqt = nn(ks.T, ds) * scale
-            dq = dqt.T.astype(BF16)
-            for i, s in enumerate(cols):
-                dq_ref[0, rsl, s] = dq[i * BLOCK : (i + 1) * BLOCK]
-            for t, val in enumerate((dk, dv)):
-                for l in range(listed):
-                    wslot[b, l, t] = val[l * BLOCK : (l + 1) * BLOCK]
-                part = val[win:]
+            keep_ds[c, b] = ds
+            stats[c, b] = (shrink * inv, dot)
+            for t, part in enumerate((nn(ds, qs) * scale, nn(pr.astype(BF16), gs))):
                 glob[t] = part if glob[t] is None else glob[t] + part
         for t in range(2):
             base = (t * heads + c) * rpp
             gpart[base : base + rpp] = glob[t].astype(BF16).reshape(rpp, PIECE, DH)
+
+    @pl.loop(0, pieces)
+    def _(i):
+        hub_send(gpart, hub2_in, hs_sem.at[2], hr_sem.at[2], lax.rem(me + i, pieces))
+
+    for c in range(heads):
+        for b in range(nb):
+            qs, gs = stacked(qv, c, b), stacked(gv, c, b)
+            ratio, dot = stats[c, b]
+            pr = keep_ex[c, b] * ratio
+            ds = (pr * (keep_dp[c, b] - dot)).astype(BF16)
+            dv = nn(pr.astype(BF16), gs)
+            dk = nn(ds, qs) * scale
+            for t, val in enumerate((dk, dv)):
+                for l in range(listed):
+                    wslot[b, l, t] = val[l * BLOCK : (l + 1) * BLOCK]
+            ks = jnp.concatenate([listed_rows(0, c, b), global_rows(gall, 0, c)], axis=0)
+            dqt = nn(ks.T, jnp.concatenate([ds, keep_ds[c, b]], axis=0)) * scale
+            dq = dqt.T.astype(BF16)
+            for i, s in enumerate(columns(c)):
+                dq_ref[0, b * BLOCK : (b + 1) * BLOCK, s] = dq[i * BLOCK : (i + 1) * BLOCK]
         for dst in range(nb + 2 * REACH):
             total = None
             for b in range(nb):
@@ -224,25 +276,22 @@
                 sback[0, c, dst - REACH - nb] = total.astype(BF16)
         for d in range(2):
             each(d, False, lambda d=d, c=c: back(d, c).start())
-        for t in range(2):
-            for r in range(rpp):
-                hub_send(gpart, hub2_in, hs_sem.at[2], hr_sem.at[2], (t * heads + c) * rpp + r)
-
-    @pl.when(me < pieces)
-    def _():
-        hub2_in[me] = gpart[me]
+
+    @pl.when(hubbed(me))
+    def _():
+        hub2_in[me] = gpart[hub]
         drain(hub2_in, n - 1, hr_sem.at[2])
         total = jnp.sum(hub2_in[...].astype(F32), axis=0).astype(BF16)
         hub2_out[...] = total
-        gall2[me] = total
+        gall2[hub] = total
 
         @pl.loop(1, n)
         def _(i):
-            remote(hub2_out, gall2.at[me], hs_sem.at[3], hr_sem.at[3], lax.rem(me + i, n)).start()
+            remote(hub2_out, gall2.at[hub], hs_sem.at[3], hr_sem.at[3], lax.rem(me + i, n)).start()
 
         drain(gall2, pieces - 1, hr_sem.at[3])
 
-    @pl.when(me >= pieces)
+    @pl.when(~hubbed(me))
     def _():
         drain(gall2, pieces, hr_sem.at[3])
 
@@ -251,8 +300,7 @@
         for d in range(2):
             each(d, True, lambda d=d, c=c: back(d, c).wait_recv())
         for t, out in enumerate((dk_ref, dv_ref)):
-            base = (t * heads + c) * rpp
-            extra = nn(hot, gall2[base : base + rpp].reshape(gtok, DH)) * flag
+            extra = nn(hot, global_rows(gall2, t, c)) * flag
             for i in range(nb):
                 rsl = slice(i * BLOCK, (i + 1) * BLOCK)
                 total = own[c, i, t] + extra[rsl]
@@ -265,14 +313,14 @@
                 each(d, False, lambda d=d, c=c, t=t: halo(d, c, t).wait_send())
             each(d, False, lambda d=d, c=c: back(d, c).wait_send())
 
-    @pl.when(me < pieces)
+    @pl.when(hubbed(me))
     def _():
         drain(gsend, pieces - 1, hs_sem.at[0])
         drain(gpart, pieces - 1, hs_sem.at[2])
         drain(hub_in, n - 1, hs_sem.at[1])
         drain(hub2_in, n - 1, hs_sem.at[3])
 
-    @pl.when(me >= pieces)
+    @pl.when(~hubbed(me))
     def _():
         drain(gsend, pieces, hs_sem.at[0])
         drain(gpart, pieces, hs_sem.at[2])
@@ -315,6 +363,9 @@
                 pltpu.VMEM((n, PIECE, DH), BF16),
                 pltpu.VMEM((PIECE, DH), BF16),
                 pltpu.VMEM((pieces, PIECE, DH), BF16),
+                pltpu.VMEM((heads, nb, listed * BLOCK, group * BLOCK), F32),
+                pltpu.VMEM((heads, nb, listed * BLOCK, group * BLOCK), F32),
+                pltpu.VMEM((heads, nb, gtok, group * BLOCK), BF16),
                 pltpu.VMEM((nb, listed + 1, 2, BLOCK, DH), F32),
                 pltpu.VMEM((heads, nb, 2, BLOCK, DH), F32),
                 pltpu.VMEM((2, heads, REACH, 2, BLOCK, DH), BF16),

time: 35 us -> 31.8 us (0.909)
  Pallas kernels: 30.6 us -> 27.4 us
    pallas_call x1, Pallas kernels: 30.6 us -> 27.4 us  [local(): pl.pallas_call(functools.partial(kernel, n, heads, group, nb, listed, gto...]
where the time goes in v2:
time: 31.8 us; the launch traced here: 31.6 us
  Pallas kernels  27.4 us (86%)
  local copies, waits for them, and re-layouts  3.51 us (11%)
  between operations  0.65 us (2%)
    pallas_call x1, Pallas kernels, local(): pl.pallas_call(functools.partial(kernel, n, heads, group, nb, listed, gto...  27.4 us
    unnamed x7, local copies, waits for them, and re-layouts  3.51 us

profile of v2, /device:TPU:0, one launch (start us, length us, event | category | flops | bytes accessed | tf_op | source)
XLA Modules:
  0.0 31.6 jit_solution(7788710483808470259)
XLA Ops:
  0.6 27.4 %shard_map.94 = (bf16[1,256,1024]{2,1,0:T(8,128)(2,1)}, bf16[1,256,256]{2,1,0:T(8,128)(2,1)}, bf16[1,256,256]{2,1,0:T(8,128)(2,1)}) custom-call(s32[16]{0:T(128)} %owner_ref.1, s32[1,2,3]{2,1,0:T(2,128)} %lists_ref.1, s32[1,64]{1,0:T(1,128)} %goff_ref.1, bf16[1,256,1024]{2,1,0:T(8,128)(2,1)} %q_hbm.1, bf16[1,256,256]{2,1,0:T(8,128)(2,1)} %k_hbm.1, ...), custom_call_target="tpu_custom_call" | custom-call | tf_op jit(solution)/shard_map/pallas_call | solution.py:346
  28.0 0.0 copy-start.1
  28.1 1.9 %copy.13 = bf16[1,256,1024]{2,1,0:T(8,128)(2,1)} copy(bf16[1,256,1024]{2,1,0:T(8,128)(2,1)} %get-tuple-element.6) | data formatting | bytes 1048576
  30.0 0.0 copy-done.1
  30.0 0.0 copy-start
  30.0 0.7 %copy.14 = bf16[1,256,256]{2,1,0:T(8,128)(2,1)} copy(bf16[1,256,256]{2,1,0:T(8,128)(2,1)S(1)} %copy-done.1) | data formatting | bytes 262144
  30.6 0.3 copy-done
  30.9 0.7 %copy.15 = bf16[1,256,256]{2,1,0:T(8,128)(2,1)} copy(bf16[1,256,256]{2,1,0:T(8,128)(2,1)S(1)} %copy-done) | data formatting | bytes 262144
Async XLA Ops:
  28.0 1.9 %copy-start.1 = (bf16[1,256,256]{2,1,0:T(8,128)(2,1)S(1)}, bf16[1,256,256]{2,1,0:T(8,128)(2,1)}, u32[]{:S(2)}) copy-start(bf16[1,256,256]{2,1,0:T(8,128)(2,1)} %get-tuple-element.7) | copy-start | bytes 393220
  30.0 1.0 %copy-start = (bf16[1,256,256]{2,1,0:T(8,128)(2,1)S(1)}, bf16[1,256,256]{2,1,0:T(8,128)(2,1)}, u32[]{:S(2)}) copy-start(bf16[1,256,256]{2,1,0:T(8,128)(2,1)} %get-tuple-element.8) | copy-start | bytes 393220

commit v3 on v2

--- a/solution.py
+++ b/solution.py
@@ -326,6 +326,16 @@
         drain(gpart, pieces, hs_sem.at[2])
 
 
+def write_out(*refs):
+    copies = [
+        pltpu.make_async_copy(refs[i], refs[3 + i], refs[6].at[i]) for i in range(3)
+    ]
+    for cp in copies:
+        cp.start()
+    for cp in copies:
+        cp.wait()
+
+
 def solution(mesh):
     n = mesh.shape["seq"]
 
@@ -343,13 +353,9 @@
         vm = pl.BlockSpec(memory_space=pltpu.VMEM)
         sm = pl.BlockSpec(memory_space=pltpu.SMEM)
         hb = pl.BlockSpec(memory_space=pl.ANY)
-        return pl.pallas_call(
+        held = pl.pallas_call(
             functools.partial(kernel, n, heads, group, nb, listed, gtok),
-            out_shape=(
-                jax.ShapeDtypeStruct(query.shape, BF16),
-                jax.ShapeDtypeStruct(keys.shape, BF16),
-                jax.ShapeDtypeStruct(values.shape, BF16),
-            ),
+            out_shape=tuple(pltpu.VMEM(a.shape, BF16) for a in (query, keys, values)),
             in_specs=[sm, sm, vm, hb, hb, hb, hb],
             out_specs=(vm, vm, vm),
             scratch_shapes=[
@@ -382,6 +388,13 @@
             + [pltpu.VMEM((wide, BLOCK, DH), BF16)] * (2 * heads),
             compiler_params=pltpu.CompilerParams(collective_id=0, has_side_effects=True),
         )(owner, block_lists, global_offset, query, keys, values, grad_out)
+        return pl.pallas_call(
+            write_out,
+            out_shape=tuple(jax.ShapeDtypeStruct(a.shape, BF16) for a in (query, keys, values)),
+            in_specs=[hb] * 3,
+            out_specs=[hb] * 3,
+            scratch_shapes=[pltpu.SemaphoreType.DMA((3,))],
+        )(*[pltpu.with_memory_space_constraint(a, pltpu.VMEM) for a in held])
 
     return jax.shard_map(
         local,

time: 31.8 us -> 28.2 us (0.89)
  local copies, waits for them, and re-layouts: 3.51 us -> 0 us
    unnamed x7 -> x0, local copies, waits for them, and re-layouts: 3.51 us -> none
    pallas_call x0 -> x1, Pallas kernels: none -> 0.9 us  [local(): pl.pallas_call(write_out, out_shape=tuple((jax.ShapeDtypeStruct(a.shape,...]
    pallas_call x1, Pallas kernels: 27.4 us -> 26.5 us  [local(): pl.pallas_call(functools.partial(kernel, n, heads, group, nb, listed, gto...]
where the time goes in v3:
time: 28.2 us; the launch traced here: 28.1 us
  Pallas kernels  27.4 us (97%)
  between operations  0.64 us (2%)
    pallas_call x1, Pallas kernels, local(): pl.pallas_call(functools.partial(kernel, n, heads, group, nb, listed, gto...  26.5 us
    pallas_call x1, Pallas kernels, local(): pl.pallas_call(write_out, out_shape=tuple((jax.ShapeDtypeStruct(a.shape,...  0.9 us

profile of v3, /device:TPU:0, one launch (start us, length us, event | category | flops | bytes accessed | tf_op | source)
XLA Modules:
  0.0 28.1 jit_solution(13753693860043119496)
XLA Ops:
  0.6 26.5 %shard_map.94 = (bf16[1,256,1024]{2,1,0:T(8,128)(2,1)S(1)}, bf16[1,256,256]{2,1,0:T(8,128)(2,1)S(1)}, bf16[1,256,256]{2,1,0:T(8,128)(2,1)S(1)}) custom-call(s32[16]{0:T(128)} %owner_ref.1, s32[1,2,3]{2,1,0:T(2,128)} %lists_ref.1, s32[1,64]{1,0:T(1,128)} %goff_ref.1, bf16[1,256,1024]{2,1,0:T(8,128)(2,1)} %q_hbm.1, bf16[1,256,256]{2,1,0:T(8,128)(2,1)} %k_hbm.1, ...), custom_call_target="tpu_custom_call" | custom-call | tf_op jit(solution)/shard_map/pallas_call | solution.py:356
  27.2 0.9 %shard_map.95 = (bf16[1,256,1024]{2,1,0:T(8,128)(2,1)}, bf16[1,256,256]{2,1,0:T(8,128)(2,1)}, bf16[1,256,256]{2,1,0:T(8,128)(2,1)}) custom-call(bf16[1,256,1024]{2,1,0:T(8,128)(2,1)S(1)} %get-tuple-element.6.refs_0_, bf16[1,256,256]{2,1,0:T(8,128)(2,1)S(1)} %get-tuple-element.7.refs_1_, bf16[1,256,256]{2,1,0:T(8,128)(2,1)S(1)} %get-tuple-element.8.refs_2_), custom_call_target="tpu_custom_call" | custom-call | tf_op jit(solution)/shard_map/pallas_call | solution.py:391

commit v4 on v3

--- a/solution.py
+++ b/solution.py
@@ -191,21 +191,20 @@
 
     stats = {}
     for c in range(heads):
-        for t in range(2):
-            for d in range(2):
-                each(d, True, lambda d=d, c=c, t=t: halo(d, c, t).wait_recv())
+        for d in range(2):
+            each(d, True, lambda d=d, c=c: halo(d, c, 0).wait_recv())
         for b in range(nb):
             st = nt(listed_rows(0, c, b), stacked(qv, c, b))
-            dp = nt(listed_rows(1, c, b), stacked(gv, c, b))
             top = jnp.max(st, axis=0, keepdims=True)
             ex = jnp.exp2((st - top) * fold)
             keep_ex[c, b] = ex
+            stats[c, b] = (top, jnp.sum(ex, axis=0, keepdims=True))
+        for d in range(2):
+            each(d, True, lambda d=d, c=c: halo(d, c, 1).wait_recv())
+        for b in range(nb):
+            dp = nt(listed_rows(1, c, b), stacked(gv, c, b))
             keep_dp[c, b] = dp
-            stats[c, b] = (
-                top,
-                jnp.sum(ex, axis=0, keepdims=True),
-                jnp.sum(ex * dp, axis=0, keepdims=True),
-            )
+            stats[c, b] += (jnp.sum(keep_ex[c, b] * dp, axis=0, keepdims=True),)
 
     @pl.when(hubbed(me))
     def _():

time: 28.2 us -> 28.7 us (1.018)
  Pallas kernels: 27.4 us -> 27.9 us
    pallas_call x1, Pallas kernels: 26.5 us -> 27 us  [local(): pl.pallas_call(functools.partial(kernel, n, heads, group, nb, listed, gto...]
where the time goes in v4:
time: 28.7 us; the launch traced here: 28.5 us
  Pallas kernels  27.9 us (97%)
  between operations  0.64 us (2%)
    pallas_call x1, Pallas kernels, local(): pl.pallas_call(functools.partial(kernel, n, heads, group, nb, listed, gto...  27 us
    pallas_call x1, Pallas kernels, local(): pl.pallas_call(write_out, out_shape=tuple((jax.ShapeDtypeStruct(a.shape,...  0.9 us

profile of v4, /device:TPU:0, one launch (start us, length us, event | category | flops | bytes accessed | tf_op | source)
XLA Modules:
  0.0 28.5 jit_solution(6967683336550542310)
XLA Ops:
  0.6 27.0 %shard_map.94 = (bf16[1,256,1024]{2,1,0:T(8,128)(2,1)S(1)}, bf16[1,256,256]{2,1,0:T(8,128)(2,1)S(1)}, bf16[1,256,256]{2,1,0:T(8,128)(2,1)S(1)}) custom-call(s32[16]{0:T(128)} %owner_ref.1, s32[1,2,3]{2,1,0:T(2,128)} %lists_ref.1, s32[1,64]{1,0:T(1,128)} %goff_ref.1, bf16[1,256,1024]{2,1,0:T(8,128)(2,1)} %q_hbm.1, bf16[1,256,256]{2,1,0:T(8,128)(2,1)} %k_hbm.1, ...), custom_call_target="tpu_custom_call" | custom-call | tf_op jit(solution)/shard_map/pallas_call | solution.py:355
  27.6 0.9 %shard_map.95 = (bf16[1,256,1024]{2,1,0:T(8,128)(2,1)}, bf16[1,256,256]{2,1,0:T(8,128)(2,1)}, bf16[1,256,256]{2,1,0:T(8,128)(2,1)}) custom-call(bf16[1,256,1024]{2,1,0:T(8,128)(2,1)S(1)} %get-tuple-element.6.refs_0_, bf16[1,256,256]{2,1,0:T(8,128)(2,1)S(1)} %get-tuple-element.7.refs_1_, bf16[1,256,256]{2,1,0:T(8,128)(2,1)S(1)} %get-tuple-element.8.refs_2_), custom_call_target="tpu_custom_call" | custom-call | tf_op jit(solution)/shard_map/pallas_call | solution.py:390
